TPU v7x, 32 devices: a whole 2x2x4 slice. The times are simulated.
32 devices in a mesh: row: 4 (over y, core), col: 8 (over z, x).
Axes of the slice: x: 2, y: 2, z: 4, core: 2. Of those that a mesh axis runs over, the one named last changes fastest.
Arguments:
- offsets: float32 [3, 8192], P(None, ('row', 'col')), may hold values from 0 to 11
- cells: int32 [3, 64], replicated, may hold values from 0 to 3, as said below
- types: int32 [8192], P(('row', 'col')), may hold values from 0 to 3, as said below
- mask: int32 [4, 16, 4, 16], P(None, 'col', 'row'), may hold values from 0 to 1, as said below
- chi_table: float32 [4], replicated, may hold values from 2 to 10.1
- eta_table: float32 [4], replicated, may hold values from 13 to 18
- gamma_table: float32 [4], replicated, may hold values from 0.4 to 0.8
Outputs:
- charges: float32 [8192], P(('row', 'col'))
Inputs may be any that keep to these rules, and one draw needn't show every extreme that they name: The cells of the blocks are a permutation of all 4 x 4 x 4 cells: each cell holds exactly one block. The mask marks a pair of blocks exactly when their cells are equal or adjacent on the periodic grid in every dimension; it is symmetric and each block is marked with exactly 27 blocks, itself included. `types`: types 2 and 3 grow more common along the atoms, from none in the first 256 atoms to nearly all in the last.
All inputs are finite; a program needn't handle non-finite values.
Results may differ from a plain program's by a relative error of at most 0.0003.
Values sent between devices are 32-bit elements; how exact they have to be, the bound alone decides.
No kernel may reach another device: no remote copies, remote signals or barrier semaphores. Data moves between devices by JAX's collectives and lax.ppermute only.
A program may use at most 64 MiB of HBM per device.

v0:
```python
import itertools
import jax
import jax.numpy as jnp
from jax import lax
from jax.experimental import pallas as pl
from jax.experimental.pallas import tpu as pltpu
from jax.sharding import PartitionSpec as P

BLOCK = 128
GRID_Z = 4
ITERS = 3

coulomb = 14.4
cutoff = 10.0
cell_side = 11.0
STEPS = tuple(itertools.product((-1, 0, 1), repeat=3))
SELF = STEPS.index((0, 0, 0))
AXES = ("row", "col")
F32 = jnp.float32


def column(row):
    return jnp.transpose(jnp.broadcast_to(row, (BLOCK, BLOCK)))


def lane_sums(acc):
    return jnp.sum(jnp.transpose(acc), axis=0, keepdims=True)


def pair_sums(vec):
    part = jnp.sum(vec.reshape(-1, 8, BLOCK), axis=0)
    part = jnp.broadcast_to(jnp.sum(part, axis=1, keepdims=True), (8, BLOCK))
    part = part + pltpu.roll(part, 4, 0)
    return part + pltpu.roll(part, 2, 0)


def scale(vec, factor):
    return (vec.reshape(-1, 8, BLOCK) * factor[None]).reshape(vec.shape)


def send_rows(out_ref, rows):
    own = jnp.concatenate(rows, axis=0)
    own = jnp.concatenate([own] * (8 // own.shape[0]), axis=0)
    out_ref[...] = jnp.broadcast_to(own[None], out_ref.shape)


def by_type(kinds, table_ref):
    out = jnp.full(kinds.shape, table_ref[0], F32)
    for kind in range(1, table_ref.shape[0]):
        out = jnp.where(kinds == float(kind), table_ref[kind], out)
    return out


def build_kernel(nb_ref, chi_ref, eta_ref, gamma_ref, geo_ref, h_ref, send_ref, rhs_ref,
                 shield_ref, tgt_ref, acc_ref):
    n_blk = shield_ref.shape[0]
    bpd = h_ref.shape[0] // len(STEPS)
    kinds = geo_ref[pl.ds(3, n_blk, stride=4), :]
    gamma = by_type(kinds, gamma_ref)
    shield_ref[...] = 1.0 / (gamma * jnp.sqrt(gamma))
    rhs_ref[pl.ds(0, n_blk, stride=2), :] = -by_type(kinds, chi_ref)
    rhs_ref[pl.ds(1, n_blk, stride=2), :] = jnp.full((n_blk, BLOCK), -1.0, F32)
    rows = []
    for own in range(bpd):
        mine = nb_ref[own * len(STEPS) + SELF]
        for comp in range(3):
            tgt_ref[comp] = column(geo_ref[pl.ds(4 * mine + comp, 1), :])
        tgt_ref[3] = column(shield_ref[pl.ds(mine, 1), :])
        acc_ref[...] = jnp.zeros(acc_ref.shape, F32)

        def pair(at, carry, own=own):
            blk = nb_ref[own * len(STEPS) + at]
            move = (at // 9 - 1, at // 3 % 3 - 1, at % 3 - 1)
            src = [
                geo_ref[pl.ds(4 * blk + comp, 1), :] + move[comp].astype(F32) * cell_side
                for comp in range(3)
            ]
            src = [jnp.broadcast_to(s, (8, BLOCK)) for s in src]
            shd = jnp.broadcast_to(shield_ref[pl.ds(blk, 1), :], (8, BLOCK))
            first = jnp.broadcast_to(rhs_ref[pl.ds(2 * blk, 1), :], (8, BLOCK))
            second = jnp.broadcast_to(rhs_ref[pl.ds(2 * blk + 1, 1), :], (8, BLOCK))
            for chunk in range(BLOCK // 8):
                at_rows = pl.ds(8 * chunk, 8)
                gap = [src[comp] - tgt_ref[comp, at_rows, :] for comp in range(3)]
                rsq = gap[0] * gap[0] + gap[1] * gap[1] + gap[2] * gap[2]
                dist = rsq * lax.rsqrt(jnp.maximum(rsq, 1e-30))
                left = jnp.maximum(cutoff - dist, 0.0)
                sq = left * left
                base = coulomb / cutoff**4
                poly = base + dist * (
                    4.0 * base / cutoff
                    + dist * (10.0 * base / cutoff**2 + dist * (20.0 * base / cutoff**3))
                )
                wide = rsq * dist + shd * tgt_ref[3, at_rows, :]
                kern = sq * sq * poly * jnp.exp2(jnp.log2(wide) * (-1.0 / 3.0))
                h_ref[own * len(STEPS) + at, at_rows, :] = kern
                acc_ref[0, at_rows, :] += kern * first
                acc_ref[1, at_rows, :] += kern * second
            return carry

        lax.fori_loop(0, len(STEPS), pair, 0)
        here = own * len(STEPS) + SELF
        diag = lax.broadcasted_iota(jnp.int32, (BLOCK, BLOCK), 0) == lax.broadcasted_iota(
            jnp.int32, (BLOCK, BLOCK), 1
        )
        eta = by_type(geo_ref[pl.ds(4 * mine + 3, 1), :], eta_ref)
        old = h_ref[here]
        new = jnp.where(diag, eta, old)
        h_ref[here] = new
        for k in range(2):
            fix = (new - old) * rhs_ref[pl.ds(2 * mine + k, 1), :]
            rows.append(lane_sums(acc_ref[k] + fix))
    send_rows(send_ref, rows)


def image_rows(nb_ref, h_ref, dir_ref):
    rows = []
    half = BLOCK // 2
    bpd = h_ref.shape[0] // len(STEPS)
    for own in range(bpd):
        parts = ([], [])
        for at_half in range(2):
            acc = [jnp.zeros((half, BLOCK), F32), jnp.zeros((half, BLOCK), F32)]
            for at in range(len(STEPS)):
                pair = own * len(STEPS) + at
                blk = nb_ref[pair]
                h = h_ref[pair, half * at_half : half * (at_half + 1), :]
                for k in range(2):
                    acc[k] = acc[k] + h * dir_ref[pl.ds(2 * blk + k, 1), :]
            for k in range(2):
                parts[k].append(acc[k])
        for k in range(2):
            rows.append(lane_sums(jnp.concatenate(parts[k], axis=0)))
    return rows


def step(image, res, direction, sol):
    norm = pair_sums(res * res)
    alpha = norm / pair_sums(direction * image)
    res = res - scale(image, alpha)
    ratio = pair_sums(res * res) / norm
    move = scale(direction, alpha)
    sol = move if sol is None else sol + move
    return res, res + scale(direction, ratio), sol


def first_kernel(nb_ref, h_ref, rhs_ref, image_ref, send_ref, res_ref, dir_ref, sol_ref):
    rhs = rhs_ref[...]
    res, direction, sol = step(image_ref[...], rhs, rhs, None)
    res_ref[...] = res
    dir_ref[...] = direction
    sol_ref[...] = sol
    send_rows(send_ref, image_rows(nb_ref, h_ref, dir_ref))


def later_kernel(nb_ref, h_ref, res_in, dir_in, sol_in, image_ref, send_ref, res_ref, dir_ref,
                 sol_ref):
    res, direction, sol = step(image_ref[...], res_in[...], dir_in[...], sol_in[...])
    res_ref[...] = res
    dir_ref[...] = direction
    sol_ref[...] = sol
    send_rows(send_ref, image_rows(nb_ref, h_ref, dir_ref))


def last_kernel(nb_ref, res_ref, dir_ref, sol_ref, image_ref, out_ref, full_ref):
    res = res_ref[...]
    direction = dir_ref[...]
    alpha = pair_sums(res * res) / pair_sums(direction * image_ref[...])
    sol = sol_ref[...] + scale(direction, alpha)
    full_ref[...] = sol
    totals = pair_sums(sol)
    ratio = totals[0:1] / totals[1:2]
    for own in range(out_ref.shape[0]):
        mine = nb_ref[own * len(STEPS) + SELF]
        out_ref[pl.ds(own, 1), :] = (
            full_ref[pl.ds(2 * mine, 1), :] - ratio * full_ref[pl.ds(2 * mine + 1, 1), :]
        )


def spread(buf, n_dev):
    rows = buf.reshape(-1, BLOCK)
    return lax.all_to_all(rows, AXES, 0, 0, tiled=True)


def per_device(offsets, cells, types, mask, chi_table, eta_table, gamma_table):
    n_row = lax.axis_size("row")
    n_col = lax.axis_size("col")
    n_dev = n_row * n_col
    me = lax.axis_index("row") * n_col + lax.axis_index("col")
    bpd = types.shape[0] // BLOCK
    n_blk = n_dev * bpd
    n_pair = bpd * len(STEPS)
    grid = jnp.array([n_row, n_col * bpd // GRID_Z, GRID_Z], jnp.int32)[:, None]

    mine = lax.dynamic_slice_in_dim(cells, me * bpd, bpd, axis=1)
    moves = jnp.array(STEPS, jnp.int32).T
    near = ((mine[:, :, None] + moves[:, None, :] + grid[:, :, None]) % grid[:, :, None])
    found = jnp.all(near.reshape(3, n_pair, 1) == cells[:, None, :], axis=0)
    nb = jnp.sum(jnp.where(found, jnp.arange(n_blk, dtype=jnp.int32)[None], 0), axis=1)

    geo = jnp.concatenate([offsets, types.astype(F32)[None]], axis=0)
    geo = geo.reshape(4, bpd, BLOCK).transpose(1, 0, 2).reshape(1, 4 * bpd, BLOCK)
    geo = spread(jnp.broadcast_to(geo, (n_dev, 4 * bpd, BLOCK)), n_dev)

    smem = pl.BlockSpec(memory_space=pltpu.SMEM)
    vmem = pl.BlockSpec(memory_space=pltpu.VMEM)
    n_vec = 2 * n_blk
    full = jax.ShapeDtypeStruct((n_vec, BLOCK), F32)
    send = jax.ShapeDtypeStruct((n_vec // 8, 8, BLOCK), F32)
    matrix, image, rhs = pl.pallas_call(
        build_kernel,
        out_shape=(pltpu.VMEM((n_pair, BLOCK, BLOCK), F32), send, full),
        in_specs=[smem] * 4 + [vmem],
        out_specs=(vmem,) * 3,
        scratch_shapes=[
            pltpu.VMEM((n_blk, BLOCK), F32),
            pltpu.VMEM((4, BLOCK, BLOCK), F32),
            pltpu.VMEM((2, BLOCK, BLOCK), F32),
        ],
        name="build",
    )(nb, chi_table, eta_table, gamma_table, geo)
    image = spread(image, n_dev)
    image, res, direction, sol = pl.pallas_call(
        first_kernel,
        out_shape=(send, full, full, full),
        in_specs=[smem] + [vmem] * 3,
        out_specs=(vmem,) * 4,
        name="first",
    )(nb, matrix, rhs, image)
    image = spread(image, n_dev)
    for _ in range(ITERS - 2):
        image, res, direction, sol = pl.pallas_call(
            later_kernel,
            out_shape=(send, full, full, full),
            in_specs=[smem] + [vmem] * 5,
            out_specs=(vmem,) * 4,
            name="later",
        )(nb, matrix, res, direction, sol, image)
        image = spread(image, n_dev)
    out = pl.pallas_call(
        last_kernel,
        out_shape=jax.ShapeDtypeStruct((bpd, BLOCK), F32),
        in_specs=[smem] + [vmem] * 4,
        out_specs=vmem,
        scratch_shapes=[pltpu.VMEM((n_vec, BLOCK), F32)],
        name="last",
    )(nb, res, direction, sol, image)
    return out.reshape(bpd * BLOCK)


def solution(mesh):
    placed = (
        P(None, AXES),
        P(),
        P(AXES),
        P(None, "col", "row", None),
        P(),
        P(),
        P(),
    )
    return jax.shard_map(
        per_device, mesh=mesh, in_specs=placed, out_specs=P(AXES), check_vma=False
    )
```

profile of v0, /device:TPU:0, one launch (start us, length us, event | category | flops | bytes accessed | tf_op | source)
XLA Modules:
  0.0 67.0 jit_solution(6822732863516881976)
XLA Ops:
  0.0 0.7 %convert_element_type.3 = f32[256]{0:T(256)S(1)} convert(s32[256]{0:T(256)} %param.11) | non-fusion elementwise | flops 256 | bytes 2048 | tf_op jit(solution)/shard_map/convert_element_type | solution.py:201
  0.7 0.7 %pad_maximum_fusion = f32[4,2,128]{2,0,1:T(4,128)S(1)} fusion(f32[1,2,128]{2,0,1:T(1,128)S(1)} %bitcast.21, f32[3,2,128]{2,0,1:T(4,128)} %bitcast.22), kind=kLoop, calls=%fused_computation.2 | loop fusion | flops 1024 | bytes 8192 | tf_op jit(solution)/shard_map/concatenate | solution.py:201
  1.4 0.6 broadcast_in_dim.27
  2.0 7.3 %all-to-all-start = ((f32[32,8,128]{2,1,0:T(8,128)}), f32[32,8,128]{2,1,0:T(8,128)S(1)}, u32[]{:S(2)}, u32[]{:S(2)}) async-start(f32[32,8,128]{2,1,0:T(8,128)} %broadcast_in_dim.27), calls=%async_computation | async-start | bytes 262144 | tf_op jit(solution)/shard_map/all_to_all | solution.py:182
  9.4 0.8 %constant_dynamic-slice_fusion = s32[3,2]{1,0:T(4,128)S(1)} fusion(s32[3,64]{1,0:T(4,128)} %param.10, s32[]{:T(128)S(6)} %select_n.21), kind=kLoop, calls=%fused_computation.8 | loop fusion | bytes 52 | tf_op jit(solution)/shard_map/dynamic_slice | solution.py:195
  10.1 0.8 %add_add_fusion = s32[3,2,27]{2,1,0:T(2,128)S(1)} fusion(s32[3,27]{1,0:T(4,128)} %constant.33, s32[3,2]{1,0:T(4,128)S(1)} %constant_dynamic-slice_fusion), kind=kLoop, calls=%fused_computation.6 | loop fusion | flops 324 | bytes 996 | tf_op jit(solution)/shard_map/add | solution.py:197
  10.9 0.1 reshape.91
  11.0 0.8 %compare_reduce_fusion = pred[54,64]{1,0:T(8,128)(4,1)S(1)} fusion(s32[3,64]{1,0:T(4,128)} %param.10, s32[3,54]{1,0:T(4,128)S(1)} %add_select_fusion), kind=kLoop, calls=%fused_computation | loop fusion | flops 17280 | bytes 4872 | tf_op jit(solution)/shard_map/reduce_and | solution.py:198
  11.8 0.6 select_reduce_fusion.nb_ref
  12.3 4.8 %all-to-all-done = f32[32,8,128]{2,1,0:T(8,128)S(1)} async-done(((f32[32,8,128]{2,1,0:T(8,128)}), f32[32,8,128]{2,1,0:T(8,128)S(1)}, u32[]{:S(2)}, u32[]{:S(2)}) %all-to-all-start) | async-done | bytes 131104 | tf_op jit(solution)/shard_map/all_to_all | solution.py:182
  17.2 0.0 copy-start.1
  17.2 0.6 copy-done.1
  17.8 7.1 %build.1 = (f32[54,128,128]{2,1,0:T(8,128)S(1)}, f32[16,8,128]{2,1,0:T(8,128)}, f32[128,128]{1,0:T(8,128)}) custom-call(s32[54]{0:T(128)} %select_reduce_fusion.nb_ref, f32[4]{0:T(128)} %chi_ref.1, f32[4]{0:T(128)} %eta_ref.1, f32[4]{0:T(128)} %gamma_ref.1, f32[256,128]{1,0:T(8,128)} %bitcast.13), custom_call_target="tpu_custom_call" | custom-call | tf_op jit(solution)/shard_map/build/pallas_call | solution.py:210
  24.9 0.0 copy-start
  24.9 1.7 %copy-done = f32[54,128,128]{2,1,0:T(8,128)} copy-done((f32[54,128,128]{2,1,0:T(8,128)}, f32[54,128,128]{2,1,0:T(8,128)S(1)}, u32[]{:S(2)}) %copy-start) | copy-done | bytes 3538968
  26.6 10.5 %all_to_all.41 = f32[32,4,128]{2,1,0:T(4,128)} all-to-all(f32[32,4,128]{2,1,0:T(4,128)} %bitcast.19), channel_id=1, replica_groups=mesh['row'=4,'col'=8] {'row','col'}, dimensions={0} | all-to-all | bytes 131072 | tf_op jit(solution)/shard_map/all_to_all | solution.py:182
  37.1 3.5 %first.1 = (f32[16,8,128]{2,1,0:T(8,128)}, f32[128,128]{1,0:T(8,128)}, f32[128,128]{1,0:T(8,128)}, f32[128,128]{1,0:T(8,128)}) custom-call(s32[54]{0:T(128)} %select_reduce_fusion.nb_ref, f32[54,128,128]{2,1,0:T(8,128)} %copy-done, f32[128,128]{1,0:T(8,128)} %get-tuple-element.17.rhs_ref, f32[128,128]{1,0:T(8,128)} %bitcast.15), custom_call_target="tpu_custom_call" | custom-call | tf_op jit(solution)/shard_map/first/pallas_call | solution.py:223
  40.6 10.5 %all_to_all.42 = f32[32,4,128]{2,1,0:T(4,128)} all-to-all(f32[32,4,128]{2,1,0:T(4,128)} %bitcast.18), channel_id=1, replica_groups=mesh['row'=4,'col'=8] {'row','col'}, dimensions={0} | all-to-all | bytes 131072 | tf_op jit(solution)/shard_map/all_to_all | solution.py:182
  51.2 3.5 %later.1 = (f32[16,8,128]{2,1,0:T(8,128)}, f32[128,128]{1,0:T(8,128)}, f32[128,128]{1,0:T(8,128)}, f32[128,128]{1,0:T(8,128)}) custom-call(s32[54]{0:T(128)} %select_reduce_fusion.nb_ref, f32[54,128,128]{2,1,0:T(8,128)} %copy-done, f32[128,128]{1,0:T(8,128)} %get-tuple-element.19.res_in, f32[128,128]{1,0:T(8,128)} %get-tuple-element.20.dir_in, ...), custom_call_target="tpu_custom_call" | custom-call | tf_op jit(solution)/shard_map/later/pallas_call | solution.py:232
  54.7 10.5 %all_to_all.43 = f32[32,4,128]{2,1,0:T(4,128)} all-to-all(f32[32,4,128]{2,1,0:T(4,128)} %bitcast.17), channel_id=1, replica_groups=mesh['row'=4,'col'=8] {'row','col'}, dimensions={0} | all-to-all | bytes 131072 | tf_op jit(solution)/shard_map/all_to_all | solution.py:182
  65.3 1.7 %last.1 = f32[2,128]{1,0:T(2,128)} custom-call(s32[54]{0:T(128)} %select_reduce_fusion.nb_ref, f32[128,128]{1,0:T(8,128)} %get-tuple-element.23.res_ref, f32[128,128]{1,0:T(8,128)} %get-tuple-element.24.dir_ref, f32[128,128]{1,0:T(8,128)} %get-tuple-element.25.sol_ref, f32[128,128]{1,0:T(8,128)} %bitcast.16), custom_call_target="tpu_custom_call" | custom-call | tf_op jit(solution)/shard_map/last/pallas_call | solution.py:240
  (1 shorter events, 0.0 us)
Async XLA Ops:
  2.0 15.1 %all-to-all-start = ((f32[32,8,128]{2,1,0:T(8,128)}), f32[32,8,128]{2,1,0:T(8,128)S(1)}, u32[]{:S(2)}, u32[]{:S(2)}) async-start(f32[32,8,128]{2,1,0:T(8,128)} %broadcast_in_dim.27), calls=%async_computation | async-start | bytes 262144 | tf_op jit(solution)/shard_map/all_to_all | solution.py:182
  17.2 0.6 copy-start.1
  24.9 1.7 %copy-start = (f32[54,128,128]{2,1,0:T(8,128)}, f32[54,128,128]{2,1,0:T(8,128)S(1)}, u32[]{:S(2)}) copy-start(f32[54,128,128]{2,1,0:T(8,128)S(1)} %get-tuple-element.16.h_ref) | copy-start | bytes 10616836
where the time goes:
time: 67.5 us; the launch traced here: 67 us
  blocking collectives  31.6 us (47%)
  Pallas kernels  15.8 us (23%)
  starting transfers between devices  7.33 us (11%)
  waiting for transfers between devices  4.81 us (7%)
  local copies, waits for them, and re-layouts  3.87 us (6%)
  other arithmetic  3.51 us (5%)
    all_to_all x3, blocking collectives, spread(): return lax.all_to_all(rows, AXES, 0, 0, tiled=True)  31.6 us
    all_to_all x1, starting transfers between devices, spread(): return lax.all_to_all(rows, AXES, 0, 0, tiled=True)  7.33 us
    pallas_call x1, Pallas kernels, per_device(): pl.pallas_call(build_kernel, out_shape=(pltpu.VMEM((n_pair, BLOCK, BLOCK)...  7.06 us
    all_to_all x1, waiting for transfers between devices, spread(): return lax.all_to_all(rows, AXES, 0, 0, tiled=True)  4.81 us
    pallas_call x1, Pallas kernels, per_device(): pl.pallas_call(later_kernel, out_shape=(send, full, full, full), in_specs...  3.54 us
    pallas_call x1, Pallas kernels, per_device(): pl.pallas_call(first_kernel, out_shape=(send, full, full, full), in_specs...  3.5 us
    unnamed x4, local copies, waits for them, and re-layouts  2.38 us
    pallas_call x1, Pallas kernels, per_device(): pl.pallas_call(last_kernel, out_shape=jax.ShapeDtypeStruct((bpd, BLOCK),...  1.72 us
  transfers between devices with their start and end apart: 1, of which 1 were waited for; matrix products, arithmetic and copies ran while one was open for 4% of the time, Pallas kernels for 0%

commit v1 on v0

--- a/solution.py
+++ b/solution.py
@@ -177,7 +177,11 @@
         )
 
 
-def spread(buf, n_dev):
+def keep(*arrays):
+    return [pltpu.with_memory_space_constraint(a, pltpu.VMEM) for a in arrays]
+
+
+def spread(buf):
     rows = buf.reshape(-1, BLOCK)
     return lax.all_to_all(rows, AXES, 0, 0, tiled=True)
 
@@ -200,13 +204,14 @@
 
     geo = jnp.concatenate([offsets, types.astype(F32)[None]], axis=0)
     geo = geo.reshape(4, bpd, BLOCK).transpose(1, 0, 2).reshape(1, 4 * bpd, BLOCK)
-    geo = spread(jnp.broadcast_to(geo, (n_dev, 4 * bpd, BLOCK)), n_dev)
+    geo = spread(jnp.broadcast_to(geo, (n_dev, 4 * bpd, BLOCK)))
 
     smem = pl.BlockSpec(memory_space=pltpu.SMEM)
     vmem = pl.BlockSpec(memory_space=pltpu.VMEM)
+    params = pltpu.CompilerParams(vmem_limit_bytes=24 * 2**20)
     n_vec = 2 * n_blk
-    full = jax.ShapeDtypeStruct((n_vec, BLOCK), F32)
-    send = jax.ShapeDtypeStruct((n_vec // 8, 8, BLOCK), F32)
+    full = pltpu.VMEM((n_vec, BLOCK), F32)
+    send = pltpu.VMEM((n_vec // 8, 8, BLOCK), F32)
     matrix, image, rhs = pl.pallas_call(
         build_kernel,
         out_shape=(pltpu.VMEM((n_pair, BLOCK, BLOCK), F32), send, full),
@@ -217,34 +222,38 @@
             pltpu.VMEM((4, BLOCK, BLOCK), F32),
             pltpu.VMEM((2, BLOCK, BLOCK), F32),
         ],
+        compiler_params=params,
         name="build",
-    )(nb, chi_table, eta_table, gamma_table, geo)
-    image = spread(image, n_dev)
+    )(nb, chi_table, eta_table, gamma_table, *keep(geo))
+    image = spread(image)
     image, res, direction, sol = pl.pallas_call(
         first_kernel,
         out_shape=(send, full, full, full),
         in_specs=[smem] + [vmem] * 3,
         out_specs=(vmem,) * 4,
+        compiler_params=params,
         name="first",
-    )(nb, matrix, rhs, image)
-    image = spread(image, n_dev)
+    )(nb, *keep(matrix, rhs, image))
+    image = spread(image)
     for _ in range(ITERS - 2):
         image, res, direction, sol = pl.pallas_call(
             later_kernel,
             out_shape=(send, full, full, full),
             in_specs=[smem] + [vmem] * 5,
             out_specs=(vmem,) * 4,
+            compiler_params=params,
             name="later",
-        )(nb, matrix, res, direction, sol, image)
-        image = spread(image, n_dev)
+        )(nb, *keep(matrix, res, direction, sol, image))
+        image = spread(image)
     out = pl.pallas_call(
         last_kernel,
         out_shape=jax.ShapeDtypeStruct((bpd, BLOCK), F32),
         in_specs=[smem] + [vmem] * 4,
         out_specs=vmem,
         scratch_shapes=[pltpu.VMEM((n_vec, BLOCK), F32)],
+        compiler_params=params,
         name="last",
-    )(nb, res, direction, sol, image)
+    )(nb, *keep(res, direction, sol, image))
     return out.reshape(bpd * BLOCK)
 
 

time: 67.5 us -> 57.1 us (0.85)
  Pallas kernels: 15.8 us -> 10.3 us
  blocking collectives: 31.6 us -> 27.4 us
    all_to_all x3, blocking collectives: 31.6 us -> 27.4 us  [spread(): return lax.all_to_all(rows, AXES, 0, 0, tiled=True)]
    pallas_call x1, Pallas kernels: 3.54 us -> 1.42 us  [per_device(): pl.pallas_call(later_kernel, out_shape=(send, full, full, full), in_specs...]
    pallas_call x1, Pallas kernels: 3.5 us -> 1.43 us  [per_device(): pl.pallas_call(first_kernel, out_shape=(send, full, full, full), in_specs...]
    pallas_call x1, Pallas kernels: 7.06 us -> 6.08 us  [per_device(): pl.pallas_call(build_kernel, out_shape=(pltpu.VMEM((n_pair, BLOCK, BLOCK)...]
    unnamed x4 -> x6, local copies, waits for them, and re-layouts: 2.38 us -> 1.96 us
where the time goes in v1:
time: 57.1 us; the launch traced here: 56.8 us
  blocking collectives  27.4 us (48%)
  Pallas kernels  10.3 us (18%)
  starting transfers between devices  7.33 us (13%)
  waiting for transfers between devices  5.3 us (9%)
  local copies, waits for them, and re-layouts  3.46 us (6%)
  other arithmetic  3.02 us (5%)
    all_to_all x3, blocking collectives, spread(): return lax.all_to_all(rows, AXES, 0, 0, tiled=True)  27.4 us
    all_to_all x1, starting transfers between devices, spread(): return lax.all_to_all(rows, AXES, 0, 0, tiled=True)  7.33 us
    pallas_call x1, Pallas kernels, per_device(): pl.pallas_call(build_kernel, out_shape=(pltpu.VMEM((n_pair, BLOCK, BLOCK)...  6.08 us
    all_to_all x1, waiting for transfers between devices, spread(): return lax.all_to_all(rows, AXES, 0, 0, tiled=True)  5.3 us
    unnamed x6, local copies, waits for them, and re-layouts  1.96 us
    pallas_call x1, Pallas kernels, per_device(): pl.pallas_call(first_kernel, out_shape=(send, full, full, full), in_specs...  1.43 us
    pallas_call x1, Pallas kernels, per_device(): pl.pallas_call(later_kernel, out_shape=(send, full, full, full), in_specs...  1.42 us
    pallas_call x1, Pallas kernels, per_device(): pl.pallas_call(last_kernel, out_shape=jax.ShapeDtypeStruct((bpd, BLOCK),...  1.31 us
  transfers between devices with their start and end apart: 1, of which 1 were waited for; matrix products, arithmetic and copies ran while one was open for 4% of the time, Pallas kernels for 0%

profile of v1, /device:TPU:0, one launch (start us, length us, event | category | flops | bytes accessed | tf_op | source)
XLA Modules:
  0.0 56.8 jit_solution(6819288591782509137)
XLA Ops:
  0.0 0.7 %convert_element_type.3 = f32[256]{0:T(256)S(1)} convert(s32[256]{0:T(256)} %param.11) | non-fusion elementwise | flops 256 | bytes 2048 | tf_op jit(solution)/shard_map/convert_element_type | solution.py:205
  0.7 0.7 %pad_maximum_fusion = f32[4,2,128]{2,0,1:T(4,128)S(1)} fusion(f32[1,2,128]{2,0,1:T(1,128)S(1)} %bitcast.21, f32[3,2,128]{2,0,1:T(4,128)} %bitcast.22), kind=kLoop, calls=%fused_computation.2 | loop fusion | flops 1024 | bytes 8192 | tf_op jit(solution)/shard_map/concatenate | solution.py:205
  1.4 0.7 %broadcast_in_dim.27 = f32[32,8,128]{2,1,0:T(8,128)} broadcast(f32[8,128]{1,0:T(8,128)S(1)} %bitcast.20), dimensions={1,2} | broadcast | bytes 135168 | tf_op jit(solution)/shard_map/broadcast_in_dim | solution.py:207
  2.0 7.3 %all-to-all-start = ((f32[32,8,128]{2,1,0:T(8,128)}), f32[32,8,128]{2,1,0:T(8,128)S(1)}, u32[]{:S(2)}, u32[]{:S(2)}) async-start(f32[32,8,128]{2,1,0:T(8,128)} %broadcast_in_dim.27), calls=%async_computation | async-start | bytes 262144 | tf_op jit(solution)/shard_map/all_to_all | solution.py:186
  9.4 0.8 %constant_dynamic-slice_fusion = s32[3,2]{1,0:T(4,128)S(1)} fusion(s32[3,64]{1,0:T(4,128)} %param.10, s32[]{:T(128)S(6)} %select_n.21), kind=kLoop, calls=%fused_computation.8 | loop fusion | bytes 52 | tf_op jit(solution)/shard_map/dynamic_slice | solution.py:199
  10.1 0.8 %add_add_fusion = s32[3,2,27]{2,1,0:T(2,128)S(1)} fusion(s32[3,27]{1,0:T(4,128)} %constant.33, s32[3,2]{1,0:T(4,128)S(1)} %constant_dynamic-slice_fusion), kind=kLoop, calls=%fused_computation.6 | loop fusion | flops 324 | bytes 996 | tf_op jit(solution)/shard_map/add | solution.py:201
  10.9 0.1 reshape.91
  11.0 0.8 %compare_reduce_fusion = pred[54,64]{1,0:T(8,128)(4,1)S(1)} fusion(s32[3,64]{1,0:T(4,128)} %param.10, s32[3,54]{1,0:T(4,128)S(1)} %add_select_fusion), kind=kLoop, calls=%fused_computation | loop fusion | flops 17280 | bytes 4872 | tf_op jit(solution)/shard_map/reduce_and | solution.py:202
  11.8 0.1 select_reduce_fusion.nb_ref
  11.9 5.3 %all-to-all-done = f32[32,8,128]{2,1,0:T(8,128)S(1)} async-done(((f32[32,8,128]{2,1,0:T(8,128)}), f32[32,8,128]{2,1,0:T(8,128)S(1)}, u32[]{:S(2)}, u32[]{:S(2)}) %all-to-all-start) | async-done | bytes 131104 | tf_op jit(solution)/shard_map/all_to_all | solution.py:186
  17.2 0.0 copy-start
  17.2 0.7 %copy-done = f32[4]{0:T(128)S(1)} copy-done((f32[4]{0:T(128)S(1)}, f32[4]{0:T(128)}, u32[]{:S(2)}) %copy-start) | copy-done | bytes 40
  17.8 0.0 copy-start.1
  17.8 0.7 %copy-done.1 = f32[4]{0:T(128)S(1)} copy-done((f32[4]{0:T(128)S(1)}, f32[4]{0:T(128)}, u32[]{:S(2)}) %copy-start.1) | copy-done | bytes 40
  18.5 0.0 copy-start.2
  18.5 0.7 %copy-done.2 = f32[4]{0:T(128)S(1)} copy-done((f32[4]{0:T(128)S(1)}, f32[4]{0:T(128)}, u32[]{:S(2)}) %copy-start.2) | copy-done | bytes 40
  19.1 6.1 %build.1 = (f32[54,128,128]{2,1,0:T(8,128)S(1)}, f32[16,8,128]{2,1,0:T(8,128)S(1)}, f32[128,128]{1,0:T(8,128)S(1)}) custom-call(s32[54]{0:T(128)S(1)} %select_reduce_fusion.nb_ref, f32[4]{0:T(128)S(1)} %copy-done, f32[4]{0:T(128)S(1)} %copy-done.1, f32[4]{0:T(128)S(1)} %copy-done.2, f32[256,128]{1,0:T(8,128)S(1)} %bitcast.13), custom_call_target="tpu_custom_call" | custom-call | tf_op jit(solution)/shard_map/build/pallas_call | solution.py:215
  25.2 9.4 %all_to_all.41 = f32[32,4,128]{2,1,0:T(4,128)S(1)} all-to-all(f32[32,4,128]{2,1,0:T(4,128)S(1)} %bitcast.19), channel_id=1, replica_groups=mesh['row'=4,'col'=8] {'row','col'}, dimensions={0} | all-to-all | bytes 131072 | tf_op jit(solution)/shard_map/all_to_all | solution.py:186
  34.7 1.4 %first.1 = (f32[16,8,128]{2,1,0:T(8,128)S(1)}, f32[128,128]{1,0:T(8,128)S(1)}, f32[128,128]{1,0:T(8,128)S(1)}, f32[128,128]{1,0:T(8,128)S(1)}) custom-call(s32[54]{0:T(128)S(1)} %select_reduce_fusion.nb_ref, f32[54,128,128]{2,1,0:T(8,128)S(1)} %get-tuple-element.16.h_ref, f32[128,128]{1,0:T(8,128)S(1)} %get-tuple-element.17.rhs_ref, f32[128,128]{1,0:T(8,128)S(1)} %bitcast.15), custom_call_target="tpu_custom_call" | custom-call | tf_op jit(solution)/shard_map/first/pallas_call | solution.py:229
  36.1 9.0 %all_to_all.42 = f32[32,4,128]{2,1,0:T(4,128)S(1)} all-to-all(f32[32,4,128]{2,1,0:T(4,128)S(1)} %bitcast.18), channel_id=1, replica_groups=mesh['row'=4,'col'=8] {'row','col'}, dimensions={0} | all-to-all | bytes 131072 | tf_op jit(solution)/shard_map/all_to_all | solution.py:186
  45.1 1.4 %later.1 = (f32[16,8,128]{2,1,0:T(8,128)S(1)}, f32[128,128]{1,0:T(8,128)S(1)}, f32[128,128]{1,0:T(8,128)S(1)}, f32[128,128]{1,0:T(8,128)S(1)}) custom-call(s32[54]{0:T(128)S(1)} %select_reduce_fusion.nb_ref, f32[54,128,128]{2,1,0:T(8,128)S(1)} %get-tuple-element.16.h_ref, f32[128,128]{1,0:T(8,128)S(1)} %get-tuple-element.19.res_in, ...), custom_call_target="tpu_custom_call" | custom-call | tf_op jit(solution)/shard_map/later/pallas_call | solution.py:239
  46.5 9.0 %all_to_all.43 = f32[32,4,128]{2,1,0:T(4,128)S(1)} all-to-all(f32[32,4,128]{2,1,0:T(4,128)S(1)} %bitcast.17), channel_id=1, replica_groups=mesh['row'=4,'col'=8] {'row','col'}, dimensions={0} | all-to-all | bytes 131072 | tf_op jit(solution)/shard_map/all_to_all | solution.py:186
  55.5 1.3 %last.1 = f32[2,128]{1,0:T(2,128)} custom-call(s32[54]{0:T(128)S(1)} %select_reduce_fusion.nb_ref, f32[128,128]{1,0:T(8,128)S(1)} %get-tuple-element.23.res_ref, f32[128,128]{1,0:T(8,128)S(1)} %get-tuple-element.24.dir_ref, f32[128,128]{1,0:T(8,128)S(1)} %get-tuple-element.25.sol_ref, f32[128,128]{1,0:T(8,128)S(1)} %bitcast.16), custom_call_target="tpu_custom_call" | custom-call | tf_op jit(solution)/shard_map/last/pallas_call | solution.py:248
  (1 shorter events, 0.0 us)
Async XLA Ops:
  2.0 15.1 %all-to-all-start = ((f32[32,8,128]{2,1,0:T(8,128)}), f32[32,8,128]{2,1,0:T(8,128)S(1)}, u32[]{:S(2)}, u32[]{:S(2)}) async-start(f32[32,8,128]{2,1,0:T(8,128)} %broadcast_in_dim.27), calls=%async_computation | async-start | bytes 262144 | tf_op jit(solution)/shard_map/all_to_all | solution.py:186
  17.2 0.7 %copy-start = (f32[4]{0:T(128)S(1)}, f32[4]{0:T(128)}, u32[]{:S(2)}) copy-start(f32[4]{0:T(128)} %chi_ref.1) | copy-start | bytes 52
  17.8 0.7 %copy-start.1 = (f32[4]{0:T(128)S(1)}, f32[4]{0:T(128)}, u32[]{:S(2)}) copy-start(f32[4]{0:T(128)} %eta_ref.1) | copy-start | bytes 52
  18.5 0.7 %copy-start.2 = (f32[4]{0:T(128)S(1)}, f32[4]{0:T(128)}, u32[]{:S(2)}) copy-start(f32[4]{0:T(128)} %gamma_ref.1) | copy-start | bytes 52

commit v2 on v1

--- a/solution.py
+++ b/solution.py
@@ -13,6 +13,8 @@
 coulomb = 14.4
 cutoff = 10.0
 cell_side = 11.0
+unit = (20.0 * coulomb / cutoff**7) ** (1.0 / 6.0)
+reach = unit * cutoff
 STEPS = tuple(itertools.product((-1, 0, 1), repeat=3))
 SELF = STEPS.index((0, 0, 0))
 AXES = ("row", "col")
@@ -44,66 +46,92 @@
     out_ref[...] = jnp.broadcast_to(own[None], out_ref.shape)
 
 
-def by_type(kinds, table_ref):
-    out = jnp.full(kinds.shape, table_ref[0], F32)
-    for kind in range(1, table_ref.shape[0]):
-        out = jnp.where(kinds == float(kind), table_ref[kind], out)
+def by_type(kinds, table_ref, which):
+    n_kind = table_ref.shape[0] // 3
+    out = jnp.full(kinds.shape, table_ref[which * n_kind], F32)
+    for kind in range(1, n_kind):
+        out = jnp.where(kinds == float(kind), table_ref[which * n_kind + kind], out)
     return out
 
 
-def build_kernel(nb_ref, chi_ref, eta_ref, gamma_ref, geo_ref, h_ref, send_ref, rhs_ref,
+def pack_kernel(offsets_in, types_in, send_ref, offsets_ref, types_ref, sems):
+    copies = [
+        pltpu.make_async_copy(offsets_in, offsets_ref, sems.at[0]),
+        pltpu.make_async_copy(types_in, types_ref, sems.at[1]),
+    ]
+    for copy in copies:
+        copy.start()
+    for copy in copies:
+        copy.wait()
+    rows = []
+    for own in range(types_ref.shape[0]):
+        at = pl.ds(own * BLOCK, BLOCK)
+        rows.append(offsets_ref[:, at])
+        rows.append(types_ref[pl.ds(own, 1), :].astype(F32))
+    send_rows(send_ref, rows)
+
+
+def build_kernel(nb_ref, table_ref, geo_ref, h_ref, send_ref, rhs_ref,
                  shield_ref, tgt_ref, acc_ref):
     n_blk = shield_ref.shape[0]
     bpd = h_ref.shape[0] // len(STEPS)
     kinds = geo_ref[pl.ds(3, n_blk, stride=4), :]
-    gamma = by_type(kinds, gamma_ref)
-    shield_ref[...] = 1.0 / (gamma * jnp.sqrt(gamma))
-    rhs_ref[pl.ds(0, n_blk, stride=2), :] = -by_type(kinds, chi_ref)
+    gamma = by_type(kinds, table_ref, 2)
+    shield_ref[...] = unit**1.5 / (gamma * jnp.sqrt(gamma))
+    rhs_ref[pl.ds(0, n_blk, stride=2), :] = -by_type(kinds, table_ref, 0)
     rhs_ref[pl.ds(1, n_blk, stride=2), :] = jnp.full((n_blk, BLOCK), -1.0, F32)
     rows = []
     for own in range(bpd):
         mine = nb_ref[own * len(STEPS) + SELF]
         for comp in range(3):
-            tgt_ref[comp] = column(geo_ref[pl.ds(4 * mine + comp, 1), :])
+            tgt_ref[comp] = column(geo_ref[pl.ds(4 * mine + comp, 1), :] * unit)
         tgt_ref[3] = column(shield_ref[pl.ds(mine, 1), :])
         acc_ref[...] = jnp.zeros(acc_ref.shape, F32)
 
-        def pair(at, carry, own=own):
-            blk = nb_ref[own * len(STEPS) + at]
-            move = (at // 9 - 1, at // 3 % 3 - 1, at % 3 - 1)
-            src = [
-                geo_ref[pl.ds(4 * blk + comp, 1), :] + move[comp].astype(F32) * cell_side
-                for comp in range(3)
-            ]
-            src = [jnp.broadcast_to(s, (8, BLOCK)) for s in src]
-            shd = jnp.broadcast_to(shield_ref[pl.ds(blk, 1), :], (8, BLOCK))
-            first = jnp.broadcast_to(rhs_ref[pl.ds(2 * blk, 1), :], (8, BLOCK))
-            second = jnp.broadcast_to(rhs_ref[pl.ds(2 * blk + 1, 1), :], (8, BLOCK))
+        def three(at, move, own=own):
+            src, shd, first = [], [], []
+            for last in range(3):
+                blk = nb_ref[own * len(STEPS) + 3 * at + last]
+                shift = (move[0], move[1], float(last - 1) * (cell_side * unit))
+                src.append([
+                    jnp.broadcast_to(
+                        geo_ref[pl.ds(4 * blk + comp, 1), :] * unit + shift[comp], (8, BLOCK)
+                    )
+                    for comp in range(3)
+                ])
+                shd.append(jnp.broadcast_to(shield_ref[pl.ds(blk, 1), :], (8, BLOCK)))
+                first.append(jnp.broadcast_to(rhs_ref[pl.ds(2 * blk, 1), :], (8, BLOCK)))
             for chunk in range(BLOCK // 8):
                 at_rows = pl.ds(8 * chunk, 8)
-                gap = [src[comp] - tgt_ref[comp, at_rows, :] for comp in range(3)]
-                rsq = gap[0] * gap[0] + gap[1] * gap[1] + gap[2] * gap[2]
-                dist = rsq * lax.rsqrt(jnp.maximum(rsq, 1e-30))
-                left = jnp.maximum(cutoff - dist, 0.0)
-                sq = left * left
-                base = coulomb / cutoff**4
-                poly = base + dist * (
-                    4.0 * base / cutoff
-                    + dist * (10.0 * base / cutoff**2 + dist * (20.0 * base / cutoff**3))
-                )
-                wide = rsq * dist + shd * tgt_ref[3, at_rows, :]
-                kern = sq * sq * poly * jnp.exp2(jnp.log2(wide) * (-1.0 / 3.0))
-                h_ref[own * len(STEPS) + at, at_rows, :] = kern
-                acc_ref[0, at_rows, :] += kern * first
-                acc_ref[1, at_rows, :] += kern * second
-            return carry
-
-        lax.fori_loop(0, len(STEPS), pair, 0)
+                tgt = [tgt_ref[comp, at_rows, :] for comp in range(4)]
+                sums = [None, None]
+                for last in range(3):
+                    gap = [src[last][comp] - tgt[comp] for comp in range(3)]
+                    rsq = gap[0] * gap[0] + gap[1] * gap[1] + gap[2] * gap[2]
+                    dist = rsq * lax.rsqrt(jnp.maximum(rsq, 1e-30))
+                    left = jnp.maximum(reach - dist, 0.0)
+                    sq = left * left
+                    poly = ((dist + 0.5 * reach) * dist + 0.2 * reach**2) * dist + 0.05 * reach**3
+                    wide = rsq * dist + shd[last] * tgt[3]
+                    kern = sq * sq * poly * jnp.exp2(jnp.log2(wide) * (-1.0 / 3.0))
+                    h_ref[own * len(STEPS) + 3 * at + last, at_rows, :] = kern
+                    part = kern * first[last]
+                    sums = [part, kern] if last == 0 else [sums[0] + part, sums[1] + kern]
+                acc_ref[0, at_rows, :] += sums[0]
+                acc_ref[1, at_rows, :] -= sums[1]
+            wrap = move[1] > 0.5 * cell_side * unit
+            return (
+                jnp.where(wrap, move[0] + cell_side * unit, move[0]),
+                jnp.where(wrap, -cell_side * unit, move[1] + cell_side * unit),
+            )
+
+        start = jnp.float32(-cell_side * unit)
+        lax.fori_loop(0, len(STEPS) // 3, three, (start, start))
         here = own * len(STEPS) + SELF
         diag = lax.broadcasted_iota(jnp.int32, (BLOCK, BLOCK), 0) == lax.broadcasted_iota(
             jnp.int32, (BLOCK, BLOCK), 1
         )
-        eta = by_type(geo_ref[pl.ds(4 * mine + 3, 1), :], eta_ref)
+        eta = by_type(geo_ref[pl.ds(4 * mine + 3, 1), :], table_ref, 1)
         old = h_ref[here]
         new = jnp.where(diag, eta, old)
         h_ref[here] = new
@@ -202,20 +230,31 @@
     found = jnp.all(near.reshape(3, n_pair, 1) == cells[:, None, :], axis=0)
     nb = jnp.sum(jnp.where(found, jnp.arange(n_blk, dtype=jnp.int32)[None], 0), axis=1)
 
-    geo = jnp.concatenate([offsets, types.astype(F32)[None]], axis=0)
-    geo = geo.reshape(4, bpd, BLOCK).transpose(1, 0, 2).reshape(1, 4 * bpd, BLOCK)
-    geo = spread(jnp.broadcast_to(geo, (n_dev, 4 * bpd, BLOCK)))
-
     smem = pl.BlockSpec(memory_space=pltpu.SMEM)
     vmem = pl.BlockSpec(memory_space=pltpu.VMEM)
     params = pltpu.CompilerParams(vmem_limit_bytes=24 * 2**20)
     n_vec = 2 * n_blk
     full = pltpu.VMEM((n_vec, BLOCK), F32)
     send = pltpu.VMEM((n_vec // 8, 8, BLOCK), F32)
+    (geo,) = pl.pallas_call(
+        pack_kernel,
+        out_shape=(pltpu.VMEM((4 * n_blk // 8, 8, BLOCK), F32),),
+        in_specs=[pl.BlockSpec(memory_space=pltpu.HBM)] * 2,
+        out_specs=(vmem,),
+        scratch_shapes=[
+            pltpu.VMEM(offsets.shape, F32),
+            pltpu.VMEM((bpd, BLOCK), jnp.int32),
+            pltpu.SemaphoreType.DMA((2,)),
+        ],
+        compiler_params=params,
+        name="pack",
+    )(offsets, types.reshape(bpd, BLOCK))
+    geo = spread(geo)
+    tables = jnp.concatenate([chi_table, eta_table, gamma_table])
     matrix, image, rhs = pl.pallas_call(
         build_kernel,
         out_shape=(pltpu.VMEM((n_pair, BLOCK, BLOCK), F32), send, full),
-        in_specs=[smem] * 4 + [vmem],
+        in_specs=[smem] * 2 + [vmem],
         out_specs=(vmem,) * 3,
         scratch_shapes=[
             pltpu.VMEM((n_blk, BLOCK), F32),
@@ -224,7 +263,7 @@
         ],
         compiler_params=params,
         name="build",
-    )(nb, chi_table, eta_table, gamma_table, *keep(geo))
+    )(nb, tables, *keep(geo))
     image = spread(image)
     image, res, direction, sol = pl.pallas_call(
         first_kernel,

time: 57.1 us -> 54 us (0.946)
  local copies, waits for them, and re-layouts: 3.46 us -> 2.21 us
  waiting for transfers between devices: 5.3 us -> 4.54 us
  other arithmetic: 3.02 us -> 2.41 us
    pallas_call x1, Pallas kernels: 6.08 us -> 4.92 us  [per_device(): pl.pallas_call(build_kernel, out_shape=(pltpu.VMEM((n_pair, BLOCK, BLOCK)...]
    all_to_all x1, waiting for transfers between devices: 5.3 us -> 4.54 us  [spread(): return lax.all_to_all(rows, AXES, 0, 0, tiled=True)]
    convert_element_type x1 -> x0, other arithmetic: 0.68 us -> none  [per_device(): geo = jnp.concatenate([offsets, types.astype(F32)[None]], axis=0)]
    pallas_call x0 -> x1, Pallas kernels: none -> 0.67 us  [per_device(): pl.pallas_call(pack_kernel, out_shape=(pltpu.VMEM((4 * n_blk // 8, 8, BLO...]
    broadcast_in_dim x1 -> x0, local copies, waits for them, and re-layouts: 0.66 us -> none  [per_device(): geo = spread(jnp.broadcast_to(geo, (n_dev, 4 * bpd, BLOCK)))]
    unnamed x6 -> x4, local copies, waits for them, and re-layouts: 1.96 us -> 1.36 us
  transfers between devices with their start and end apart: 1 -> 1, of which waited for: 1 -> 1; matrix products, arithmetic and copies ran while one was open for 4% -> 6% of each run, Pallas kernels for 0% -> 0%
where the time goes in v2:
time: 54 us; the launch traced here: 53.7 us
  blocking collectives  27.4 us (51%)
  Pallas kernels  9.75 us (18%)
  starting transfers between devices  7.33 us (14%)
  waiting for transfers between devices  4.54 us (8%)
  other arithmetic  2.41 us (4%)
  local copies, waits for them, and re-layouts  2.21 us (4%)
    all_to_all x3, blocking collectives, spread(): return lax.all_to_all(rows, AXES, 0, 0, tiled=True)  27.4 us
    all_to_all x1, starting transfers between devices, spread(): return lax.all_to_all(rows, AXES, 0, 0, tiled=True)  7.33 us
    pallas_call x1, Pallas kernels, per_device(): pl.pallas_call(build_kernel, out_shape=(pltpu.VMEM((n_pair, BLOCK, BLOCK)...  4.92 us
    all_to_all x1, waiting for transfers between devices, spread(): return lax.all_to_all(rows, AXES, 0, 0, tiled=True)  4.54 us
    pallas_call x1, Pallas kernels, per_device(): pl.pallas_call(first_kernel, out_shape=(send, full, full, full), in_specs...  1.42 us
    pallas_call x1, Pallas kernels, per_device(): pl.pallas_call(later_kernel, out_shape=(send, full, full, full), in_specs...  1.42 us
    unnamed x4, local copies, waits for them, and re-layouts  1.36 us
    pallas_call x1, Pallas kernels, per_device(): pl.pallas_call(last_kernel, out_shape=jax.ShapeDtypeStruct((bpd, BLOCK),...  1.31 us
  transfers between devices with their start and end apart: 1, of which 1 were waited for; matrix products, arithmetic and copies ran while one was open for 6% of the time, Pallas kernels for 0%

profile of v2, /device:TPU:0, one launch (start us, length us, event | category | flops | bytes accessed | tf_op | source)
XLA Modules:
  0.0 53.7 jit_solution(6244493703765131700)
XLA Ops:
  0.0 0.0 copy-start
  0.0 0.7 %copy-done = f32[3,256]{1,0:T(4,128)S(1)} copy-done((f32[3,256]{1,0:T(4,128)S(1)}, f32[3,256]{1,0:T(4,128)}, u32[]{:S(2)}) %copy-start) | copy-done | bytes 3096
  0.7 0.0 copy-start.1
  0.7 0.7 %copy-done.1 = s32[256]{0:T(256)S(1)} copy-done((s32[256]{0:T(256)S(1)}, s32[256]{0:T(256)}, u32[]{:S(2)}) %copy-start.1) | copy-done | bytes 1048
  1.4 0.7 %pack.1 = f32[32,8,128]{2,1,0:T(8,128)} custom-call(f32[3,256]{1,0:T(4,128)S(1)} %copy-done, s32[2,128]{1,0:T(2,128)S(1)} %bitcast.16), custom_call_target="tpu_custom_call" | custom-call | tf_op jit(solution)/shard_map/pack/pallas_call | solution.py:239
  2.0 7.3 %all-to-all-start = ((f32[32,8,128]{2,1,0:T(8,128)}), f32[32,8,128]{2,1,0:T(8,128)S(1)}, u32[]{:S(2)}, u32[]{:S(2)}) async-start(f32[32,8,128]{2,1,0:T(8,128)} %pack.1), calls=%async_computation | async-start | bytes 262144 | tf_op jit(solution)/shard_map/all_to_all | solution.py:214
  9.4 0.8 %constant_dynamic-slice_fusion = s32[3,2]{1,0:T(4,128)S(1)} fusion(s32[3,64]{1,0:T(4,128)} %param.10, s32[]{:T(128)S(6)} %select_n.21), kind=kLoop, calls=%fused_computation.8 | loop fusion | bytes 52 | tf_op jit(solution)/shard_map/dynamic_slice | solution.py:227
  10.1 0.8 %add_add_fusion = s32[3,2,27]{2,1,0:T(2,128)S(1)} fusion(s32[3,27]{1,0:T(4,128)} %constant.33, s32[3,2]{1,0:T(4,128)S(1)} %constant_dynamic-slice_fusion), kind=kLoop, calls=%fused_computation.5 | loop fusion | flops 324 | bytes 996 | tf_op jit(solution)/shard_map/add | solution.py:229
  10.9 0.1 reshape.89
  11.0 0.8 %pad_maximum_fusion.table_ref = f32[12]{0:T(128)S(1)} fusion(f32[4]{0:T(128)} %param.14, f32[4]{0:T(128)} %param.13, f32[4]{0:T(128)} %param.12), kind=kLoop, calls=%fused_computation.7 | loop fusion | flops 24 | bytes 96 | tf_op jit(solution)/shard_map/concatenate | solution.py:253
  11.8 0.8 %compare_reduce_fusion = pred[54,64]{1,0:T(8,128)(4,1)S(1)} fusion(s32[3,64]{1,0:T(4,128)} %param.10, s32[3,54]{1,0:T(4,128)S(1)} %add_select_fusion), kind=kLoop, calls=%fused_computation | loop fusion | flops 17280 | bytes 4872 | tf_op jit(solution)/shard_map/reduce_and | solution.py:230
  12.5 0.1 select_reduce_fusion.nb_ref
  12.7 4.5 %all-to-all-done = f32[32,8,128]{2,1,0:T(8,128)S(1)} async-done(((f32[32,8,128]{2,1,0:T(8,128)}), f32[32,8,128]{2,1,0:T(8,128)S(1)}, u32[]{:S(2)}, u32[]{:S(2)}) %all-to-all-start) | async-done | bytes 131104 | tf_op jit(solution)/shard_map/all_to_all | solution.py:214
  17.2 4.9 %build.1 = (f32[54,128,128]{2,1,0:T(8,128)S(1)}, f32[16,8,128]{2,1,0:T(8,128)S(1)}, f32[128,128]{1,0:T(8,128)S(1)}) custom-call(s32[54]{0:T(128)S(1)} %select_reduce_fusion.nb_ref, f32[12]{0:T(128)S(1)} %pad_maximum_fusion.table_ref, f32[256,128]{1,0:T(8,128)S(1)} %bitcast.9), custom_call_target="tpu_custom_call" | custom-call | tf_op jit(solution)/shard_map/build/pallas_call | solution.py:254
  22.1 9.4 %all_to_all.41 = f32[32,4,128]{2,1,0:T(4,128)S(1)} all-to-all(f32[32,4,128]{2,1,0:T(4,128)S(1)} %bitcast.15), channel_id=1, replica_groups=mesh['row'=4,'col'=8] {'row','col'}, dimensions={0} | all-to-all | bytes 131072 | tf_op jit(solution)/shard_map/all_to_all | solution.py:214
  31.6 1.4 %first.1 = (f32[16,8,128]{2,1,0:T(8,128)S(1)}, f32[128,128]{1,0:T(8,128)S(1)}, f32[128,128]{1,0:T(8,128)S(1)}, f32[128,128]{1,0:T(8,128)S(1)}) custom-call(s32[54]{0:T(128)S(1)} %select_reduce_fusion.nb_ref, f32[54,128,128]{2,1,0:T(8,128)S(1)} %get-tuple-element.16.h_ref, f32[128,128]{1,0:T(8,128)S(1)} %get-tuple-element.17.rhs_ref, f32[128,128]{1,0:T(8,128)S(1)} %bitcast.11), custom_call_target="tpu_custom_call" | custom-call | tf_op jit(solution)/shard_map/first/pallas_call | solution.py:268
  33.0 9.0 %all_to_all.42 = f32[32,4,128]{2,1,0:T(4,128)S(1)} all-to-all(f32[32,4,128]{2,1,0:T(4,128)S(1)} %bitcast.14), channel_id=1, replica_groups=mesh['row'=4,'col'=8] {'row','col'}, dimensions={0} | all-to-all | bytes 131072 | tf_op jit(solution)/shard_map/all_to_all | solution.py:214
  42.0 1.4 %later.1 = (f32[16,8,128]{2,1,0:T(8,128)S(1)}, f32[128,128]{1,0:T(8,128)S(1)}, f32[128,128]{1,0:T(8,128)S(1)}, f32[128,128]{1,0:T(8,128)S(1)}) custom-call(s32[54]{0:T(128)S(1)} %select_reduce_fusion.nb_ref, f32[54,128,128]{2,1,0:T(8,128)S(1)} %get-tuple-element.16.h_ref, f32[128,128]{1,0:T(8,128)S(1)} %get-tuple-element.19.res_in, ...), custom_call_target="tpu_custom_call" | custom-call | tf_op jit(solution)/shard_map/later/pallas_call | solution.py:278
  43.4 9.0 %all_to_all.43 = f32[32,4,128]{2,1,0:T(4,128)S(1)} all-to-all(f32[32,4,128]{2,1,0:T(4,128)S(1)} %bitcast.13), channel_id=1, replica_groups=mesh['row'=4,'col'=8] {'row','col'}, dimensions={0} | all-to-all | bytes 131072 | tf_op jit(solution)/shard_map/all_to_all | solution.py:214
  52.4 1.3 %last.1 = f32[2,128]{1,0:T(2,128)} custom-call(s32[54]{0:T(128)S(1)} %select_reduce_fusion.nb_ref, f32[128,128]{1,0:T(8,128)S(1)} %get-tuple-element.23.res_ref, f32[128,128]{1,0:T(8,128)S(1)} %get-tuple-element.24.dir_ref, f32[128,128]{1,0:T(8,128)S(1)} %get-tuple-element.25.sol_ref, f32[128,128]{1,0:T(8,128)S(1)} %bitcast.12), custom_call_target="tpu_custom_call" | custom-call | tf_op jit(solution)/shard_map/last/pallas_call | solution.py:287
  (1 shorter events, 0.0 us)
Async XLA Ops:
  0.0 0.7 %copy-start = (f32[3,256]{1,0:T(4,128)S(1)}, f32[3,256]{1,0:T(4,128)}, u32[]{:S(2)}) copy-start(f32[3,256]{1,0:T(4,128)} %offsets_in.1) | copy-start | bytes 9220
  0.7 0.7 %copy-start.1 = (s32[256]{0:T(256)S(1)}, s32[256]{0:T(256)}, u32[]{:S(2)}) copy-start(s32[256]{0:T(256)} %param.11) | copy-start | bytes 3076
  2.0 15.1 %all-to-all-start = ((f32[32,8,128]{2,1,0:T(8,128)}), f32[32,8,128]{2,1,0:T(8,128)S(1)}, u32[]{:S(2)}, u32[]{:S(2)}) async-start(f32[32,8,128]{2,1,0:T(8,128)} %pack.1), calls=%async_computation | async-start | bytes 262144 | tf_op jit(solution)/shard_map/all_to_all | solution.py:214

commit v3 on v2

--- a/solution.py
+++ b/solution.py
@@ -190,19 +190,34 @@
     send_rows(send_ref, image_rows(nb_ref, h_ref, dir_ref))
 
 
-def last_kernel(nb_ref, res_ref, dir_ref, sol_ref, image_ref, out_ref, full_ref):
-    res = res_ref[...]
-    direction = dir_ref[...]
-    alpha = pair_sums(res * res) / pair_sums(direction * image_ref[...])
-    sol = sol_ref[...] + scale(direction, alpha)
-    full_ref[...] = sol
-    totals = pair_sums(sol)
+def final_kernel(nb_ref, h_ref, res_in, dir_in, sol_in, image_ref, send_ref, dir_ref, stats_ref,
+                 own_ref, sol_ref):
+    res, direction, sol = step(image_ref[...], res_in[...], dir_in[...], sol_in[...])
+    dir_ref[...] = direction
+    sol_ref[...] = sol
+    for at, vec in enumerate((res * res, sol, direction)):
+        stats_ref[at] = pair_sums(vec)
+    bpd = h_ref.shape[0] // len(STEPS)
+    for own in range(bpd):
+        mine = nb_ref[own * len(STEPS) + SELF]
+        for k in range(2):
+            own_ref[pl.ds(2 * own + k, 1), :] = sol_ref[pl.ds(2 * mine + k, 1), :]
+            own_ref[pl.ds(2 * (bpd + own) + k, 1), :] = dir_ref[pl.ds(2 * mine + k, 1), :]
+    send_rows(send_ref, image_rows(nb_ref, h_ref, dir_ref))
+
+
+def last_kernel(dir_ref, stats_ref, own_ref, image_ref, out_ref):
+    alpha = stats_ref[0] / pair_sums(dir_ref[...] * image_ref[...])
+    totals = stats_ref[1] + alpha * stats_ref[2]
     ratio = totals[0:1] / totals[1:2]
-    for own in range(out_ref.shape[0]):
-        mine = nb_ref[own * len(STEPS) + SELF]
-        out_ref[pl.ds(own, 1), :] = (
-            full_ref[pl.ds(2 * mine, 1), :] - ratio * full_ref[pl.ds(2 * mine + 1, 1), :]
-        )
+    bpd = out_ref.shape[0]
+    for own in range(bpd):
+        first, second = [
+            own_ref[pl.ds(2 * own + k, 1), :]
+            + alpha[k : k + 1] * own_ref[pl.ds(2 * (bpd + own) + k, 1), :]
+            for k in range(2)
+        ]
+        out_ref[pl.ds(own, 1), :] = first - ratio * second
 
 
 def keep(*arrays):
@@ -248,7 +263,10 @@
         ],
         compiler_params=params,
         name="pack",
-    )(offsets, types.reshape(bpd, BLOCK))
+    )(*[
+        pltpu.with_memory_space_constraint(a, pltpu.HBM)
+        for a in (offsets, types.reshape(bpd, BLOCK))
+    ])
     geo = spread(geo)
     tables = jnp.concatenate([chi_table, eta_table, gamma_table])
     matrix, image, rhs = pl.pallas_call(
@@ -274,7 +292,7 @@
         name="first",
     )(nb, *keep(matrix, rhs, image))
     image = spread(image)
-    for _ in range(ITERS - 2):
+    for _ in range(ITERS - 3):
         image, res, direction, sol = pl.pallas_call(
             later_kernel,
             out_shape=(send, full, full, full),
@@ -284,15 +302,28 @@
             name="later",
         )(nb, *keep(matrix, res, direction, sol, image))
         image = spread(image)
+    image, direction, stats, own = pl.pallas_call(
+        final_kernel,
+        out_shape=(
+            send,
+            full,
+            pltpu.VMEM((3, 8, BLOCK), F32),
+            pltpu.VMEM((4 * bpd, BLOCK), F32),
+        ),
+        in_specs=[smem] + [vmem] * 5,
+        out_specs=(vmem,) * 4,
+        scratch_shapes=[pltpu.VMEM((n_vec, BLOCK), F32)],
+        compiler_params=params,
+        name="final",
+    )(nb, *keep(matrix, res, direction, sol, image))
     out = pl.pallas_call(
         last_kernel,
         out_shape=jax.ShapeDtypeStruct((bpd, BLOCK), F32),
-        in_specs=[smem] + [vmem] * 4,
+        in_specs=[vmem] * 4,
         out_specs=vmem,
-        scratch_shapes=[pltpu.VMEM((n_vec, BLOCK), F32)],
         compiler_params=params,
         name="last",
-    )(nb, *keep(res, direction, sol, image))
+    )(*keep(direction, stats, own, spread(image)))
     return out.reshape(bpd * BLOCK)
 
 

time: 54 us -> 52.9 us (0.980)
  local copies, waits for them, and re-layouts: 2.21 us -> 0.84 us
    unnamed x4 -> x0, local copies, waits for them, and re-layouts: 1.36 us -> none
    pallas_call x1, Pallas kernels: 0.67 us -> 1.36 us  [per_device(): pl.pallas_call(pack_kernel, out_shape=(pltpu.VMEM((4 * n_blk // 8, 8, BLO...]
    pallas_call x1, Pallas kernels: 1.31 us -> 0.68 us  [per_device(): pl.pallas_call(last_kernel, out_shape=jax.ShapeDtypeStruct((bpd, BLOCK),...]
where the time goes in v3:
time: 52.9 us; the launch traced here: 52.5 us
  blocking collectives  27.4 us (52%)
  Pallas kernels  9.95 us (19%)
  starting transfers between devices  7.33 us (14%)
  waiting for transfers between devices  4.54 us (9%)
  other arithmetic  2.41 us (5%)
  local copies, waits for them, and re-layouts  0.84 us (2%)
    all_to_all x3, blocking collectives, spread(): return lax.all_to_all(rows, AXES, 0, 0, tiled=True)  27.4 us
    all_to_all x1, starting transfers between devices, spread(): return lax.all_to_all(rows, AXES, 0, 0, tiled=True)  7.33 us
    pallas_call x1, Pallas kernels, per_device(): pl.pallas_call(build_kernel, out_shape=(pltpu.VMEM((n_pair, BLOCK, BLOCK)...  4.92 us
    all_to_all x1, waiting for transfers between devices, spread(): return lax.all_to_all(rows, AXES, 0, 0, tiled=True)  4.54 us
    pallas_call x1, Pallas kernels, per_device(): pl.pallas_call(final_kernel, out_shape=(send, full, pltpu.VMEM((3, 8, BLO...  1.57 us
    pallas_call x1, Pallas kernels, per_device(): pl.pallas_call(first_kernel, out_shape=(send, full, full, full), in_specs...  1.43 us
    pallas_call x1, Pallas kernels, per_device(): pl.pallas_call(pack_kernel, out_shape=(pltpu.VMEM((4 * n_blk // 8, 8, BLO...  1.36 us
  transfers between devices with their start and end apart: 1, of which 1 were waited for; matrix products, arithmetic and copies ran while one was open for 6% of the time, Pallas kernels for 0%

profile of v3, /device:TPU:0, one launch (start us, length us, event | category | flops | bytes accessed | tf_op | source)
XLA Modules:
  0.0 52.5 jit_solution(12763733461042007407)
XLA Ops:
  0.0 1.4 %pack.1 = f32[32,8,128]{2,1,0:T(8,128)} custom-call(f32[3,256]{1,0:T(4,128)} %offsets_in.1, s32[2,128]{1,0:T(2,128)} %bitcast.16), custom_call_target="tpu_custom_call" | custom-call | tf_op jit(solution)/shard_map/pack/pallas_call | solution.py:254
  1.4 7.3 %all-to-all-start = ((f32[32,8,128]{2,1,0:T(8,128)}), f32[32,8,128]{2,1,0:T(8,128)S(1)}, u32[]{:S(2)}, u32[]{:S(2)}) async-start(f32[32,8,128]{2,1,0:T(8,128)} %pack.1), calls=%async_computation | async-start | bytes 262144 | tf_op jit(solution)/shard_map/all_to_all | solution.py:229
  8.7 0.8 %constant_dynamic-slice_fusion = s32[3,2]{1,0:T(4,128)S(1)} fusion(s32[3,64]{1,0:T(4,128)} %param.10, s32[]{:T(128)S(6)} %select_n.21), kind=kLoop, calls=%fused_computation.8 | loop fusion | bytes 52 | tf_op jit(solution)/shard_map/dynamic_slice | solution.py:242
  9.5 0.8 %add_add_fusion = s32[3,2,27]{2,1,0:T(2,128)S(1)} fusion(s32[3,27]{1,0:T(4,128)} %constant.33, s32[3,2]{1,0:T(4,128)S(1)} %constant_dynamic-slice_fusion), kind=kLoop, calls=%fused_computation.5 | loop fusion | flops 324 | bytes 996 | tf_op jit(solution)/shard_map/add | solution.py:244
  10.2 0.1 reshape.89
  10.3 0.8 %pad_maximum_fusion.table_ref = f32[12]{0:T(128)S(1)} fusion(f32[4]{0:T(128)} %param.14, f32[4]{0:T(128)} %param.13, f32[4]{0:T(128)} %param.12), kind=kLoop, calls=%fused_computation.7 | loop fusion | flops 24 | bytes 96 | tf_op jit(solution)/shard_map/concatenate | solution.py:271
  11.1 0.8 %compare_reduce_fusion = pred[54,64]{1,0:T(8,128)(4,1)S(1)} fusion(s32[3,64]{1,0:T(4,128)} %param.10, s32[3,54]{1,0:T(4,128)S(1)} %add_select_fusion), kind=kLoop, calls=%fused_computation | loop fusion | flops 17280 | bytes 4872 | tf_op jit(solution)/shard_map/reduce_and | solution.py:245
  11.9 0.1 select_reduce_fusion.nb_ref
  12.0 4.5 %all-to-all-done = f32[32,8,128]{2,1,0:T(8,128)S(1)} async-done(((f32[32,8,128]{2,1,0:T(8,128)}), f32[32,8,128]{2,1,0:T(8,128)S(1)}, u32[]{:S(2)}, u32[]{:S(2)}) %all-to-all-start) | async-done | bytes 131104 | tf_op jit(solution)/shard_map/all_to_all | solution.py:229
  16.5 4.9 %build.1 = (f32[54,128,128]{2,1,0:T(8,128)S(1)}, f32[16,8,128]{2,1,0:T(8,128)S(1)}, f32[128,128]{1,0:T(8,128)S(1)}) custom-call(s32[54]{0:T(128)S(1)} %select_reduce_fusion.nb_ref, f32[12]{0:T(128)S(1)} %pad_maximum_fusion.table_ref, f32[256,128]{1,0:T(8,128)S(1)} %bitcast.9), custom_call_target="tpu_custom_call" | custom-call | tf_op jit(solution)/shard_map/build/pallas_call | solution.py:272
  21.4 9.4 %all_to_all.41 = f32[32,4,128]{2,1,0:T(4,128)S(1)} all-to-all(f32[32,4,128]{2,1,0:T(4,128)S(1)} %bitcast.15), channel_id=1, replica_groups=mesh['row'=4,'col'=8] {'row','col'}, dimensions={0} | all-to-all | bytes 131072 | tf_op jit(solution)/shard_map/all_to_all | solution.py:229
  30.9 1.4 %first.1 = (f32[16,8,128]{2,1,0:T(8,128)S(1)}, f32[128,128]{1,0:T(8,128)S(1)}, f32[128,128]{1,0:T(8,128)S(1)}, f32[128,128]{1,0:T(8,128)S(1)}) custom-call(s32[54]{0:T(128)S(1)} %select_reduce_fusion.nb_ref, f32[54,128,128]{2,1,0:T(8,128)S(1)} %get-tuple-element.16.h_ref, f32[128,128]{1,0:T(8,128)S(1)} %get-tuple-element.17.rhs_ref, f32[128,128]{1,0:T(8,128)S(1)} %bitcast.11), custom_call_target="tpu_custom_call" | custom-call | tf_op jit(solution)/shard_map/first/pallas_call | solution.py:286
  32.3 9.0 %all_to_all.42 = f32[32,4,128]{2,1,0:T(4,128)S(1)} all-to-all(f32[32,4,128]{2,1,0:T(4,128)S(1)} %bitcast.14), channel_id=1, replica_groups=mesh['row'=4,'col'=8] {'row','col'}, dimensions={0} | all-to-all | bytes 131072 | tf_op jit(solution)/shard_map/all_to_all | solution.py:229
  41.3 1.6 %final.1 = (f32[16,8,128]{2,1,0:T(8,128)S(1)}, f32[128,128]{1,0:T(8,128)S(1)}, f32[3,8,128]{2,1,0:T(8,128)S(1)}, f32[8,128]{1,0:T(8,128)S(1)}) custom-call(s32[54]{0:T(128)S(1)} %select_reduce_fusion.nb_ref, f32[54,128,128]{2,1,0:T(8,128)S(1)} %get-tuple-element.16.h_ref, f32[128,128]{1,0:T(8,128)S(1)} %get-tuple-element.19.res_in, ...), custom_call_target="tpu_custom_call" | custom-call | tf_op jit(solution)/shard_map/final/pallas_call | solution.py:305
  42.9 9.0 %all_to_all.43 = f32[32,4,128]{2,1,0:T(4,128)S(1)} all-to-all(f32[32,4,128]{2,1,0:T(4,128)S(1)} %bitcast.13), channel_id=1, replica_groups=mesh['row'=4,'col'=8] {'row','col'}, dimensions={0} | all-to-all | bytes 131072 | tf_op jit(solution)/shard_map/all_to_all | solution.py:229
  51.8 0.7 %last.1 = f32[2,128]{1,0:T(2,128)} custom-call(f32[128,128]{1,0:T(8,128)S(1)} %get-tuple-element.23.dir_ref, f32[3,8,128]{2,1,0:T(8,128)S(1)} %get-tuple-element.24.stats_ref, f32[8,128]{1,0:T(8,128)S(1)} %get-tuple-element.25.own_ref, f32[128,128]{1,0:T(8,128)S(1)} %bitcast.12), custom_call_target="tpu_custom_call" | custom-call | tf_op jit(solution)/shard_map/last/pallas_call | solution.py:319
  (1 shorter events, 0.0 us)
Async XLA Ops:
  1.4 15.1 %all-to-all-start = ((f32[32,8,128]{2,1,0:T(8,128)}), f32[32,8,128]{2,1,0:T(8,128)S(1)}, u32[]{:S(2)}, u32[]{:S(2)}) async-start(f32[32,8,128]{2,1,0:T(8,128)} %pack.1), calls=%async_computation | async-start | bytes 262144 | tf_op jit(solution)/shard_map/all_to_all | solution.py:229

commit v4 on v3

--- a/solution.py
+++ b/solution.py
@@ -17,6 +17,7 @@
 reach = unit * cutoff
 STEPS = tuple(itertools.product((-1, 0, 1), repeat=3))
 SELF = STEPS.index((0, 0, 0))
+PLANE = len(STEPS) // 3
 AXES = ("row", "col")
 F32 = jnp.float32
 
@@ -88,11 +89,11 @@
         tgt_ref[3] = column(shield_ref[pl.ds(mine, 1), :])
         acc_ref[...] = jnp.zeros(acc_ref.shape, F32)
 
-        def three(at, move, own=own):
+        def plane(at, move, own=own):
             src, shd, first = [], [], []
-            for last in range(3):
-                blk = nb_ref[own * len(STEPS) + 3 * at + last]
-                shift = (move[0], move[1], float(last - 1) * (cell_side * unit))
+            for last in range(PLANE):
+                blk = nb_ref[own * len(STEPS) + PLANE * at + last]
+                shift = (move,) + tuple(float(s) * (cell_side * unit) for s in STEPS[last][1:])
                 src.append([
                     jnp.broadcast_to(
                         geo_ref[pl.ds(4 * blk + comp, 1), :] * unit + shift[comp], (8, BLOCK)
@@ -105,7 +106,7 @@
                 at_rows = pl.ds(8 * chunk, 8)
                 tgt = [tgt_ref[comp, at_rows, :] for comp in range(4)]
                 sums = [None, None]
-                for last in range(3):
+                for last in range(PLANE):
                     gap = [src[last][comp] - tgt[comp] for comp in range(3)]
                     rsq = gap[0] * gap[0] + gap[1] * gap[1] + gap[2] * gap[2]
                     dist = rsq * lax.rsqrt(jnp.maximum(rsq, 1e-30))
@@ -114,19 +115,14 @@
                     poly = ((dist + 0.5 * reach) * dist + 0.2 * reach**2) * dist + 0.05 * reach**3
                     wide = rsq * dist + shd[last] * tgt[3]
                     kern = sq * sq * poly * jnp.exp2(jnp.log2(wide) * (-1.0 / 3.0))
-                    h_ref[own * len(STEPS) + 3 * at + last, at_rows, :] = kern
+                    h_ref[own * len(STEPS) + PLANE * at + last, at_rows, :] = kern
                     part = kern * first[last]
                     sums = [part, kern] if last == 0 else [sums[0] + part, sums[1] + kern]
                 acc_ref[0, at_rows, :] += sums[0]
                 acc_ref[1, at_rows, :] -= sums[1]
-            wrap = move[1] > 0.5 * cell_side * unit
-            return (
-                jnp.where(wrap, move[0] + cell_side * unit, move[0]),
-                jnp.where(wrap, -cell_side * unit, move[1] + cell_side * unit),
-            )
-
-        start = jnp.float32(-cell_side * unit)
-        lax.fori_loop(0, len(STEPS) // 3, three, (start, start))
+            return move + cell_side * unit
+
+        lax.fori_loop(0, len(STEPS) // PLANE, plane, jnp.float32(-cell_side * unit))
         here = own * len(STEPS) + SELF
         diag = lax.broadcasted_iota(jnp.int32, (BLOCK, BLOCK), 0) == lax.broadcasted_iota(
             jnp.int32, (BLOCK, BLOCK), 1

time: 52.9 us -> 52.6 us (level)
  no operation moved by 1% of the time
where the time goes in v4:
time: 52.6 us; the launch traced here: 52.3 us
  blocking collectives  27.4 us (52%)
  Pallas kernels  9.7 us (18%)
  starting transfers between devices  7.33 us (14%)
  waiting for transfers between devices  4.54 us (9%)
  other arithmetic  2.41 us (5%)
  local copies, waits for them, and re-layouts  0.84 us (2%)
    all_to_all x3, blocking collectives, spread(): return lax.all_to_all(rows, AXES, 0, 0, tiled=True)  27.4 us
    all_to_all x1, starting transfers between devices, spread(): return lax.all_to_all(rows, AXES, 0, 0, tiled=True)  7.33 us
    pallas_call x1, Pallas kernels, per_device(): pl.pallas_call(build_kernel, out_shape=(pltpu.VMEM((n_pair, BLOCK, BLOCK)...  4.68 us
    all_to_all x1, waiting for transfers between devices, spread(): return lax.all_to_all(rows, AXES, 0, 0, tiled=True)  4.54 us
    pallas_call x1, Pallas kernels, per_device(): pl.pallas_call(final_kernel, out_shape=(send, full, pltpu.VMEM((3, 8, BLO...  1.56 us
    pallas_call x1, Pallas kernels, per_device(): pl.pallas_call(first_kernel, out_shape=(send, full, full, full), in_specs...  1.42 us
    pallas_call x1, Pallas kernels, per_device(): pl.pallas_call(pack_kernel, out_shape=(pltpu.VMEM((4 * n_blk // 8, 8, BLO...  1.36 us
  transfers between devices with their start and end apart: 1, of which 1 were waited for; matrix products, arithmetic and copies ran while one was open for 6% of the time, Pallas kernels for 0%

profile of v4, /device:TPU:0, one launch (start us, length us, event | category | flops | bytes accessed | tf_op | source)
XLA Modules:
  0.0 52.3 jit_solution(16582025919574693924)
XLA Ops:
  0.0 1.4 %pack.1 = f32[32,8,128]{2,1,0:T(8,128)} custom-call(f32[3,256]{1,0:T(4,128)} %offsets_in.1, s32[2,128]{1,0:T(2,128)} %bitcast.16), custom_call_target="tpu_custom_call" | custom-call | tf_op jit(solution)/shard_map/pack/pallas_call | solution.py:250
  1.4 7.3 %all-to-all-start = ((f32[32,8,128]{2,1,0:T(8,128)}), f32[32,8,128]{2,1,0:T(8,128)S(1)}, u32[]{:S(2)}, u32[]{:S(2)}) async-start(f32[32,8,128]{2,1,0:T(8,128)} %pack.1), calls=%async_computation | async-start | bytes 262144 | tf_op jit(solution)/shard_map/all_to_all | solution.py:225
  8.7 0.8 %constant_dynamic-slice_fusion = s32[3,2]{1,0:T(4,128)S(1)} fusion(s32[3,64]{1,0:T(4,128)} %param.10, s32[]{:T(128)S(6)} %select_n.21), kind=kLoop, calls=%fused_computation.8 | loop fusion | bytes 52 | tf_op jit(solution)/shard_map/dynamic_slice | solution.py:238
  9.5 0.8 %add_add_fusion = s32[3,2,27]{2,1,0:T(2,128)S(1)} fusion(s32[3,27]{1,0:T(4,128)} %constant.33, s32[3,2]{1,0:T(4,128)S(1)} %constant_dynamic-slice_fusion), kind=kLoop, calls=%fused_computation.5 | loop fusion | flops 324 | bytes 996 | tf_op jit(solution)/shard_map/add | solution.py:240
  10.2 0.1 reshape.89
  10.3 0.8 %pad_maximum_fusion.table_ref = f32[12]{0:T(128)S(1)} fusion(f32[4]{0:T(128)} %param.14, f32[4]{0:T(128)} %param.13, f32[4]{0:T(128)} %param.12), kind=kLoop, calls=%fused_computation.7 | loop fusion | flops 24 | bytes 96 | tf_op jit(solution)/shard_map/concatenate | solution.py:267
  11.1 0.8 %compare_reduce_fusion = pred[54,64]{1,0:T(8,128)(4,1)S(1)} fusion(s32[3,64]{1,0:T(4,128)} %param.10, s32[3,54]{1,0:T(4,128)S(1)} %add_select_fusion), kind=kLoop, calls=%fused_computation | loop fusion | flops 17280 | bytes 4872 | tf_op jit(solution)/shard_map/reduce_and | solution.py:241
  11.9 0.1 select_reduce_fusion.nb_ref
  12.0 4.5 %all-to-all-done = f32[32,8,128]{2,1,0:T(8,128)S(1)} async-done(((f32[32,8,128]{2,1,0:T(8,128)}), f32[32,8,128]{2,1,0:T(8,128)S(1)}, u32[]{:S(2)}, u32[]{:S(2)}) %all-to-all-start) | async-done | bytes 131104 | tf_op jit(solution)/shard_map/all_to_all | solution.py:225
  16.5 4.7 %build.1 = (f32[54,128,128]{2,1,0:T(8,128)S(1)}, f32[16,8,128]{2,1,0:T(8,128)S(1)}, f32[128,128]{1,0:T(8,128)S(1)}) custom-call(s32[54]{0:T(128)S(1)} %select_reduce_fusion.nb_ref, f32[12]{0:T(128)S(1)} %pad_maximum_fusion.table_ref, f32[256,128]{1,0:T(8,128)S(1)} %bitcast.9), custom_call_target="tpu_custom_call" | custom-call | tf_op jit(solution)/shard_map/build/pallas_call | solution.py:268
  21.2 9.4 %all_to_all.41 = f32[32,4,128]{2,1,0:T(4,128)S(1)} all-to-all(f32[32,4,128]{2,1,0:T(4,128)S(1)} %bitcast.15), channel_id=1, replica_groups=mesh['row'=4,'col'=8] {'row','col'}, dimensions={0} | all-to-all | bytes 131072 | tf_op jit(solution)/shard_map/all_to_all | solution.py:225
  30.6 1.4 %first.1 = (f32[16,8,128]{2,1,0:T(8,128)S(1)}, f32[128,128]{1,0:T(8,128)S(1)}, f32[128,128]{1,0:T(8,128)S(1)}, f32[128,128]{1,0:T(8,128)S(1)}) custom-call(s32[54]{0:T(128)S(1)} %select_reduce_fusion.nb_ref, f32[54,128,128]{2,1,0:T(8,128)S(1)} %get-tuple-element.16.h_ref, f32[128,128]{1,0:T(8,128)S(1)} %get-tuple-element.17.rhs_ref, f32[128,128]{1,0:T(8,128)S(1)} %bitcast.11), custom_call_target="tpu_custom_call" | custom-call | tf_op jit(solution)/shard_map/first/pallas_call | solution.py:282
  32.1 9.0 %all_to_all.42 = f32[32,4,128]{2,1,0:T(4,128)S(1)} all-to-all(f32[32,4,128]{2,1,0:T(4,128)S(1)} %bitcast.14), channel_id=1, replica_groups=mesh['row'=4,'col'=8] {'row','col'}, dimensions={0} | all-to-all | bytes 131072 | tf_op jit(solution)/shard_map/all_to_all | solution.py:225
  41.0 1.6 %final.1 = (f32[16,8,128]{2,1,0:T(8,128)S(1)}, f32[128,128]{1,0:T(8,128)S(1)}, f32[3,8,128]{2,1,0:T(8,128)S(1)}, f32[8,128]{1,0:T(8,128)S(1)}) custom-call(s32[54]{0:T(128)S(1)} %select_reduce_fusion.nb_ref, f32[54,128,128]{2,1,0:T(8,128)S(1)} %get-tuple-element.16.h_ref, f32[128,128]{1,0:T(8,128)S(1)} %get-tuple-element.19.res_in, ...), custom_call_target="tpu_custom_call" | custom-call | tf_op jit(solution)/shard_map/final/pallas_call | solution.py:301
  42.6 9.0 %all_to_all.43 = f32[32,4,128]{2,1,0:T(4,128)S(1)} all-to-all(f32[32,4,128]{2,1,0:T(4,128)S(1)} %bitcast.13), channel_id=1, replica_groups=mesh['row'=4,'col'=8] {'row','col'}, dimensions={0} | all-to-all | bytes 131072 | tf_op jit(solution)/shard_map/all_to_all | solution.py:225
  51.6 0.7 %last.1 = f32[2,128]{1,0:T(2,128)} custom-call(f32[128,128]{1,0:T(8,128)S(1)} %get-tuple-element.23.dir_ref, f32[3,8,128]{2,1,0:T(8,128)S(1)} %get-tuple-element.24.stats_ref, f32[8,128]{1,0:T(8,128)S(1)} %get-tuple-element.25.own_ref, f32[128,128]{1,0:T(8,128)S(1)} %bitcast.12), custom_call_target="tpu_custom_call" | custom-call | tf_op jit(solution)/shard_map/last/pallas_call | solution.py:315
  (1 shorter events, 0.0 us)
Async XLA Ops:
  1.4 15.1 %all-to-all-start = ((f32[32,8,128]{2,1,0:T(8,128)}), f32[32,8,128]{2,1,0:T(8,128)S(1)}, u32[]{:S(2)}, u32[]{:S(2)}) async-start(f32[32,8,128]{2,1,0:T(8,128)} %pack.1), calls=%async_computation | async-start | bytes 262144 | tf_op jit(solution)/shard_map/all_to_all | solution.py:225

commit v5 on v4

--- a/solution.py
+++ b/solution.py
@@ -139,11 +139,11 @@
 
 def image_rows(nb_ref, h_ref, dir_ref):
     rows = []
-    half = BLOCK // 2
+    half = BLOCK
     bpd = h_ref.shape[0] // len(STEPS)
     for own in range(bpd):
         parts = ([], [])
-        for at_half in range(2):
+        for at_half in range(BLOCK // half):
             acc = [jnp.zeros((half, BLOCK), F32), jnp.zeros((half, BLOCK), F32)]
             for at in range(len(STEPS)):
                 pair = own * len(STEPS) + at

time: 52.6 us -> 52.6 us (level)
  no operation moved by 1% of the time
where the time goes in v5:
time: 52.6 us; the launch traced here: 52.3 us
  blocking collectives  27.4 us (52%)
  Pallas kernels  9.7 us (18%)
  starting transfers between devices  7.33 us (14%)
  waiting for transfers between devices  4.54 us (9%)
  other arithmetic  2.41 us (5%)
  local copies, waits for them, and re-layouts  0.84 us (2%)
    all_to_all x3, blocking collectives, spread(): return lax.all_to_all(rows, AXES, 0, 0, tiled=True)  27.4 us
    all_to_all x1, starting transfers between devices, spread(): return lax.all_to_all(rows, AXES, 0, 0, tiled=True)  7.33 us
    pallas_call x1, Pallas kernels, per_device(): pl.pallas_call(build_kernel, out_shape=(pltpu.VMEM((n_pair, BLOCK, BLOCK)...  4.68 us
    all_to_all x1, waiting for transfers between devices, spread(): return lax.all_to_all(rows, AXES, 0, 0, tiled=True)  4.54 us
    pallas_call x1, Pallas kernels, per_device(): pl.pallas_call(final_kernel, out_shape=(send, full, pltpu.VMEM((3, 8, BLO...  1.56 us
    pallas_call x1, Pallas kernels, per_device(): pl.pallas_call(first_kernel, out_shape=(send, full, full, full), in_specs...  1.42 us
    pallas_call x1, Pallas kernels, per_device(): pl.pallas_call(pack_kernel, out_shape=(pltpu.VMEM((4 * n_blk // 8, 8, BLO...  1.36 us
  transfers between devices with their start and end apart: 1, of which 1 were waited for; matrix products, arithmetic and copies ran while one was open for 6% of the time, Pallas kernels for 0%

profile of v5, /device:TPU:0, one launch (start us, length us, event | category | flops | bytes accessed | tf_op | source)
XLA Modules:
  0.0 52.3 jit_solution(16582025919574693924)
XLA Ops:
  0.0 1.4 %pack.1 = f32[32,8,128]{2,1,0:T(8,128)} custom-call(f32[3,256]{1,0:T(4,128)} %offsets_in.1, s32[2,128]{1,0:T(2,128)} %bitcast.16), custom_call_target="tpu_custom_call" | custom-call | tf_op jit(solution)/shard_map/pack/pallas_call | solution.py:250
  1.4 7.3 %all-to-all-start = ((f32[32,8,128]{2,1,0:T(8,128)}), f32[32,8,128]{2,1,0:T(8,128)S(1)}, u32[]{:S(2)}, u32[]{:S(2)}) async-start(f32[32,8,128]{2,1,0:T(8,128)} %pack.1), calls=%async_computation | async-start | bytes 262144 | tf_op jit(solution)/shard_map/all_to_all | solution.py:225
  8.7 0.8 %constant_dynamic-slice_fusion = s32[3,2]{1,0:T(4,128)S(1)} fusion(s32[3,64]{1,0:T(4,128)} %param.10, s32[]{:T(128)S(6)} %select_n.21), kind=kLoop, calls=%fused_computation.8 | loop fusion | bytes 52 | tf_op jit(solution)/shard_map/dynamic_slice | solution.py:238
  9.5 0.8 %add_add_fusion = s32[3,2,27]{2,1,0:T(2,128)S(1)} fusion(s32[3,27]{1,0:T(4,128)} %constant.33, s32[3,2]{1,0:T(4,128)S(1)} %constant_dynamic-slice_fusion), kind=kLoop, calls=%fused_computation.5 | loop fusion | flops 324 | bytes 996 | tf_op jit(solution)/shard_map/add | solution.py:240
  10.2 0.1 reshape.89
  10.3 0.8 %pad_maximum_fusion.table_ref = f32[12]{0:T(128)S(1)} fusion(f32[4]{0:T(128)} %param.14, f32[4]{0:T(128)} %param.13, f32[4]{0:T(128)} %param.12), kind=kLoop, calls=%fused_computation.7 | loop fusion | flops 24 | bytes 96 | tf_op jit(solution)/shard_map/concatenate | solution.py:267
  11.1 0.8 %compare_reduce_fusion = pred[54,64]{1,0:T(8,128)(4,1)S(1)} fusion(s32[3,64]{1,0:T(4,128)} %param.10, s32[3,54]{1,0:T(4,128)S(1)} %add_select_fusion), kind=kLoop, calls=%fused_computation | loop fusion | flops 17280 | bytes 4872 | tf_op jit(solution)/shard_map/reduce_and | solution.py:241
  11.9 0.1 select_reduce_fusion.nb_ref
  12.0 4.5 %all-to-all-done = f32[32,8,128]{2,1,0:T(8,128)S(1)} async-done(((f32[32,8,128]{2,1,0:T(8,128)}), f32[32,8,128]{2,1,0:T(8,128)S(1)}, u32[]{:S(2)}, u32[]{:S(2)}) %all-to-all-start) | async-done | bytes 131104 | tf_op jit(solution)/shard_map/all_to_all | solution.py:225
  16.5 4.7 %build.1 = (f32[54,128,128]{2,1,0:T(8,128)S(1)}, f32[16,8,128]{2,1,0:T(8,128)S(1)}, f32[128,128]{1,0:T(8,128)S(1)}) custom-call(s32[54]{0:T(128)S(1)} %select_reduce_fusion.nb_ref, f32[12]{0:T(128)S(1)} %pad_maximum_fusion.table_ref, f32[256,128]{1,0:T(8,128)S(1)} %bitcast.9), custom_call_target="tpu_custom_call" | custom-call | tf_op jit(solution)/shard_map/build/pallas_call | solution.py:268
  21.2 9.4 %all_to_all.41 = f32[32,4,128]{2,1,0:T(4,128)S(1)} all-to-all(f32[32,4,128]{2,1,0:T(4,128)S(1)} %bitcast.15), channel_id=1, replica_groups=mesh['row'=4,'col'=8] {'row','col'}, dimensions={0} | all-to-all | bytes 131072 | tf_op jit(solution)/shard_map/all_to_all | solution.py:225
  30.6 1.4 %first.1 = (f32[16,8,128]{2,1,0:T(8,128)S(1)}, f32[128,128]{1,0:T(8,128)S(1)}, f32[128,128]{1,0:T(8,128)S(1)}, f32[128,128]{1,0:T(8,128)S(1)}) custom-call(s32[54]{0:T(128)S(1)} %select_reduce_fusion.nb_ref, f32[54,128,128]{2,1,0:T(8,128)S(1)} %get-tuple-element.16.h_ref, f32[128,128]{1,0:T(8,128)S(1)} %get-tuple-element.17.rhs_ref, f32[128,128]{1,0:T(8,128)S(1)} %bitcast.11), custom_call_target="tpu_custom_call" | custom-call | tf_op jit(solution)/shard_map/first/pallas_call | solution.py:282
  32.1 9.0 %all_to_all.42 = f32[32,4,128]{2,1,0:T(4,128)S(1)} all-to-all(f32[32,4,128]{2,1,0:T(4,128)S(1)} %bitcast.14), channel_id=1, replica_groups=mesh['row'=4,'col'=8] {'row','col'}, dimensions={0} | all-to-all | bytes 131072 | tf_op jit(solution)/shard_map/all_to_all | solution.py:225
  41.0 1.6 %final.1 = (f32[16,8,128]{2,1,0:T(8,128)S(1)}, f32[128,128]{1,0:T(8,128)S(1)}, f32[3,8,128]{2,1,0:T(8,128)S(1)}, f32[8,128]{1,0:T(8,128)S(1)}) custom-call(s32[54]{0:T(128)S(1)} %select_reduce_fusion.nb_ref, f32[54,128,128]{2,1,0:T(8,128)S(1)} %get-tuple-element.16.h_ref, f32[128,128]{1,0:T(8,128)S(1)} %get-tuple-element.19.res_in, ...), custom_call_target="tpu_custom_call" | custom-call | tf_op jit(solution)/shard_map/final/pallas_call | solution.py:301
  42.6 9.0 %all_to_all.43 = f32[32,4,128]{2,1,0:T(4,128)S(1)} all-to-all(f32[32,4,128]{2,1,0:T(4,128)S(1)} %bitcast.13), channel_id=1, replica_groups=mesh['row'=4,'col'=8] {'row','col'}, dimensions={0} | all-to-all | bytes 131072 | tf_op jit(solution)/shard_map/all_to_all | solution.py:225
  51.6 0.7 %last.1 = f32[2,128]{1,0:T(2,128)} custom-call(f32[128,128]{1,0:T(8,128)S(1)} %get-tuple-element.23.dir_ref, f32[3,8,128]{2,1,0:T(8,128)S(1)} %get-tuple-element.24.stats_ref, f32[8,128]{1,0:T(8,128)S(1)} %get-tuple-element.25.own_ref, f32[128,128]{1,0:T(8,128)S(1)} %bitcast.12), custom_call_target="tpu_custom_call" | custom-call | tf_op jit(solution)/shard_map/last/pallas_call | solution.py:315
  (1 shorter events, 0.0 us)
Async XLA Ops:
  1.4 15.1 %all-to-all-start = ((f32[32,8,128]{2,1,0:T(8,128)}), f32[32,8,128]{2,1,0:T(8,128)S(1)}, u32[]{:S(2)}, u32[]{:S(2)}) async-start(f32[32,8,128]{2,1,0:T(8,128)} %pack.1), calls=%async_computation | async-start | bytes 262144 | tf_op jit(solution)/shard_map/all_to_all | solution.py:225
